TPU v7x, 32 devices: a whole 2x2x4 slice. The times are simulated.
32 devices in a mesh: gx: 2 (over x), gy: 4 (over y, core), gz: 4 (over z).
Axes of the slice: x: 2, y: 2, z: 4, core: 2. Of those that a mesh axis runs over, the one named last changes fastest.
Arguments:
- state: float32 [5, 12, 96, 1536], P(None, 'gx', 'gy', 'gz'), as said below
- register: float32 [5, 12, 96, 1536], P(None, 'gx', 'gy', 'gz'), may hold values from -0.25 to 0.25
Outputs:
- new_state: float32 [5, 12, 96, 1536], P(None, 'gx', 'gy', 'gz')
- new_register: float32 [5, 12, 96, 1536], P(None, 'gx', 'gy', 'gz')
Inputs may be any that keep to these rules, and one draw needn't show every extreme that they name: Density is between 0.5 and 2.5, and the pressure computed from the state is positive.
All inputs are finite; a program needn't handle non-finite values.
Results may differ from a plain program's by a relative error of at most 0.0003.
Values sent between devices are 32-bit elements; how exact they have to be, the bound alone decides.
A program may use at most 128 MiB of HBM per device.

v0:
```python
import functools
import math

import jax
import jax.numpy as jnp
import numpy as np
from jax import lax
from jax.experimental import pallas as pl
from jax.experimental.pallas import tpu as pltpu
from jax.sharding import PartitionSpec as P

GAMMA = 1.4
GM1 = 0.4
ELEM_WIDTH = 0.05
COURANT = 0.5
INV_W = 15.0
SCALE = 2.0 / ELEM_WIDTH
HALF = 0.5 * INV_W * SCALE
COEFFS = (
    (-567301805773.0 / 1357537059087.0, 5161836677717.0 / 13612068292357.0),
    (-2404267990393.0 / 2016746695238.0, 1720146321549.0 / 2090206949498.0),
)
AXES = ("gx", "gy", "gz")
NV = 5
SUB = 8
LANE = 128
MESH = pl.DeviceIdType.MESH


def gll_derivative():
    seven = math.sqrt(7.0)
    inner = math.sqrt(1.0 / 3.0 - 2.0 * seven / 21.0)
    outer = math.sqrt(1.0 / 3.0 + 2.0 * seven / 21.0)
    points = np.array([-1.0, -outer, -inner, inner, outer, 1.0])
    count = len(points)
    weights = np.array(
        [np.prod([points[i] - points[j] for j in range(count) if j != i]) for i in range(count)]
    )
    table = np.zeros((count, count))
    for i in range(count):
        for j in range(count):
            if i != j:
                table[i, j] = weights[i] / weights[j] / (points[i] - points[j])
        table[i, i] = -np.sum(table[i])
    return table


DMAT = gll_derivative()
NODES = DMAT.shape[0]


def operator(length):
    op = np.kron(np.eye(length // NODES), -SCALE * DMAT)
    for j in range(NODES, length, NODES):
        i = j - 1
        op[j, j] -= HALF
        op[j, i] += HALF
        op[i, j] -= HALF
        op[i, i] += HALF
    op[np.abs(op) < 1e-9] = 0.0
    return op


def split(table):
    high = np.asarray(table, np.float32).astype(jnp.bfloat16)
    low = (np.asarray(table, np.float32) - high.astype(np.float32)).astype(jnp.bfloat16)
    return np.stack([high, low])


def windows(length):
    op = operator(length).T
    count = length // LANE - 1
    out = np.zeros((count, 2 * LANE, 2 * LANE))
    for w in range(count):
        lo = 0 if w == 0 else LANE // 2
        hi = 2 * LANE if w == count - 1 else LANE + LANE // 2
        base = w * LANE
        out[w, :, lo:hi] = op[base : base + 2 * LANE, base + lo : base + hi]
    return out


def primitives(u):
    inv = 1.0 / u[0]
    mom_sq = u[1] * u[1] + u[2] * u[2] + u[3] * u[3]
    press = GM1 * (u[4] - 0.5 * mom_sq * inv)
    sound = jnp.sqrt(GAMMA * press * inv)
    return inv, mom_sq, press, sound


def flux_of(u, d, inv, press):
    vel = u[1 + d] * inv
    parts = [u[1 + d], u[1] * vel, u[2] * vel, u[3] * vel, (u[4] + press) * vel]
    parts[1 + d] = parts[1 + d] + press
    return parts, vel


def face_terms(low, up, d):
    inv_l, _, press_l, sound_l = primitives(low)
    inv_u, _, press_u, sound_u = primitives(up)
    flux_l, vel_l = flux_of(low, d, inv_l, press_l)
    flux_u, vel_u = flux_of(up, d, inv_u, press_u)
    lam = jnp.maximum(jnp.abs(vel_l) + sound_l, jnp.abs(vel_u) + sound_u)
    first, last = [], []
    for v in range(NV):
        central = HALF * (flux_u[v] - flux_l[v])
        jump = (HALF * lam) * (up[v] - low[v])
        first.append(-central - jump)
        last.append(jump - central)
    return first, last


def kernel(
    dims, sizes,
    state_ref, reg_ref, ly_ref, wz_ref, out_ref, reg_out_ref,
    u1_ref, acc_ref, fx_ref, fy_ref, fz_ref, sy_ref, sz_ref, step_ref,
    xh_ref, yp_ref, yh_ref, zp_ref, zh_ref, mcur_ref, mx_ref,
    xs_sem, xr_sem, ys_sem, yr_sem, zs_sem, zr_sem, ms_sem, mr_sem,
):
    nx, ny, nz = dims
    rows = nx * ny
    tiles = ny // SUB
    me = [lax.axis_index(a) for a in AXES]

    def peer(axis, offset):
        n = sizes[axis]
        return {AXES[axis]: lax.rem(me[axis] + (offset % n), n)}

    barrier = pltpu.get_barrier_semaphore()
    greeted = 0
    for axis in range(3):
        for off in range(1, sizes[axis]):
            pl.semaphore_signal(barrier, inc=1, device_id=peer(axis, off), device_id_type=MESH)
            greeted += 1
    pl.semaphore_wait(barrier, greeted)

    def remote(src, dst, ssem, rsem, axis, off):
        return pltpu.make_async_remote_copy(
            src_ref=src, dst_ref=dst, send_sem=ssem, recv_sem=rsem,
            device_id=peer(axis, off), device_id_type=MESH,
        )

    def x_copy(u_ref, sec, side, t):
        base = (rows - ny if side == 0 else 0) + t * SUB
        return remote(
            u_ref.at[:, pl.ds(base, SUB), :], xh_ref.at[sec, side, :, pl.ds(t * SUB, SUB), :],
            xs_sem.at[sec, side, t], xr_sem.at[sec, side, t], 0, 1 if side == 0 else -1,
        )

    def y_copy(sec, side):
        return remote(
            yp_ref.at[sec, 1 - side], yh_ref.at[sec, side],
            ys_sem.at[sec, side], yr_sem.at[sec, side], 1, 1 if side == 0 else -1,
        )

    def z_copy(sec, side):
        return remote(
            zp_ref.at[sec, 1 - side], zh_ref.at[sec, side],
            zs_sem.at[sec, side], zr_sem.at[sec, side], 2, 1 if side == 0 else -1,
        )

    def m_copy(axis, off):
        return remote(
            mcur_ref.at[axis], mx_ref.at[axis, off],
            ms_sem.at[axis, off], mr_sem.at[axis, off], axis, off,
        )

    lane_ids = lax.broadcasted_iota(jnp.int32, (ny, LANE), 1)

    def pack(u_ref, sec):
        for v in range(NV):
            for x in range(nx):
                a = x * ny
                yp_ref[sec, 0, v, x : x + 1, :] = u_ref[v, a : a + 1, :]
                yp_ref[sec, 1, v, x : x + 1, :] = u_ref[v, a + ny - 1 : a + ny, :]

        def one(v, carry):
            first = jnp.ones((ny, LANE), jnp.float32)
            last = first
            for x in range(nx):
                r = slice(x * ny, x * ny + ny)
                first = jnp.where(lane_ids == x, u_ref[v, r, 0:LANE][:, 0:1], first)
                last = jnp.where(lane_ids == x, u_ref[v, r, nz - LANE : nz][:, LANE - 1 : LANE], last)
            zp_ref[sec, 0, v] = first
            zp_ref[sec, 1, v] = last
            return carry

        lax.fori_loop(0, NV, one, 0)

    def pointwise(u_ref, want_max):
        def one(t, top):
            r = pl.ds(pl.multiple_of(t * SUB, SUB), SUB)
            u = [u_ref[v, r, :] for v in range(NV)]
            inv, mom_sq, press, sound = primitives(u)
            for d, f_ref in enumerate((fx_ref, fy_ref, fz_ref)):
                parts, vel = flux_of(u, d, inv, press)
                for v in range(NV):
                    f_ref[v, r, :] = parts[v]
                if d == 1:
                    sy_ref[r, :] = jnp.abs(vel) + sound
                if d == 2:
                    sz_ref[r, :] = jnp.abs(vel) + sound
            if want_max:
                speed = jnp.sqrt(mom_sq) * inv + sound
                for b in range(nz // LANE):
                    top = jnp.maximum(top, speed[:, b * LANE : (b + 1) * LANE])
            return top

        return lax.fori_loop(0, rows // SUB, one, jnp.zeros((SUB, LANE), jnp.float32))

    def halves(x):
        high = x.astype(jnp.bfloat16)
        return high, (x - high.astype(jnp.float32)).astype(jnp.bfloat16)

    def dot(a, b):
        return jnp.dot(a, b, preferred_element_type=jnp.float32)

    def products(v, carry):
        high, low = halves(fy_ref[v])
        acc_ref[v] = dot(ly_ref[0], high) + dot(ly_ref[0], low) + dot(ly_ref[1], high)
        high, low = halves(fz_ref[v])
        for w in range(nz // LANE - 1):
            c = slice(w * LANE, (w + 2) * LANE)
            acc_ref[v, :, c] += (
                dot(high[:, c], wz_ref[0, w]) + dot(low[:, c], wz_ref[0, w]) + dot(high[:, c], wz_ref[1, w])
            )
        return carry

    op_x = operator(nx)

    def along_x(t, carry):
        v = lax.div(t, tiles)
        base = lax.rem(t, tiles) * SUB
        where = [pl.ds(pl.multiple_of(base + i * ny, SUB), SUB) for i in range(nx)]
        f = [fx_ref[v, r, :] for r in where]
        for i in range(nx):
            total = acc_ref[v, where[i], :]
            for j in range(nx):
                if op_x[i, j] != 0.0:
                    total = total + float(op_x[i, j]) * f[j]
            acc_ref[v, where[i], :] = total
        return carry

    row_in = lax.broadcasted_iota(jnp.int32, (ny, nz), 0)
    lane_in = lax.broadcasted_iota(jnp.int32, (ny, nz), 1)

    def dissipate(u_ref):
        def one(x, carry):
            r = pl.ds(pl.multiple_of(x * ny, SUB), ny)
            s = sy_ref[r, :]
            mask = (lax.rem(row_in, NODES) == 0) & (row_in > 0)
            lam_y = jnp.where(mask, HALF * jnp.maximum(s, pltpu.roll(s, 1, 0)), 0.0)
            s = sz_ref[r, :]
            mask = (lax.rem(lane_in, NODES) == 0) & (lane_in > 0)
            lam_z = jnp.where(mask, HALF * jnp.maximum(s, pltpu.roll(s, 1, 1)), 0.0)
            for v in range(NV):
                u = u_ref[v, r, :]
                wy = lam_y * (u - pltpu.roll(u, 1, 0))
                wz = lam_z * (u - pltpu.roll(u, 1, 1))
                acc_ref[v, r, :] += (pltpu.roll(wy, ny - 1, 0) - wy) + (pltpu.roll(wz, nz - 1, 1) - wz)
            return carry

        lax.fori_loop(0, nx, one, 0)
        for e in range(NODES, nx, NODES):
            lo, up = (e - 1) * ny, e * ny
            for t in range(tiles):
                ra = slice(lo + t * SUB, lo + t * SUB + SUB)
                rb = slice(up + t * SUB, up + t * SUB + SUB)
                a = [u_ref[v, ra, :] for v in range(NV)]
                b = [u_ref[v, rb, :] for v in range(NV)]
                ia, _, _, ca = primitives(a)
                ib, _, _, cb = primitives(b)
                lam = HALF * jnp.maximum(jnp.abs(a[1] * ia) + ca, jnp.abs(b[1] * ib) + cb)
                for v in range(NV):
                    jump = lam * (b[v] - a[v])
                    acc_ref[v, rb, :] -= jump
                    acc_ref[v, ra, :] += jump

    def volume(u_ref):
        lax.fori_loop(0, NV, products, 0)
        lax.fori_loop(0, NV * tiles, along_x, 0)
        dissipate(u_ref)

    def edges_y(sec):
        for side in range(2):
            y_copy(sec, side).wait_recv()
            own = [yp_ref[sec, side, v] for v in range(NV)]
            other = [yh_ref[sec, side, v] for v in range(NV)]
            corr = face_terms(other, own, 1)[0] if side == 0 else face_terms(own, other, 1)[1]
            for v in range(NV):
                for x in range(nx):
                    a = x * ny + (0 if side == 0 else ny - 1)
                    acc_ref[v, a : a + 1, :] += corr[v][x : x + 1, :]

    def edges_z(sec):
        for side in range(2):
            z_copy(sec, side).wait_recv()
            own = [zp_ref[sec, side, v] for v in range(NV)]
            other = [zh_ref[sec, side, v] for v in range(NV)]
            corr = face_terms(other, own, 2)[0] if side == 0 else face_terms(own, other, 2)[1]
            at = 0 if side == 0 else LANE - 1
            c = slice(0, LANE) if side == 0 else slice(nz - LANE, nz)
            for v in range(NV):
                for x in range(nx):
                    r = slice(x * ny, x * ny + ny)
                    acc_ref[v, r, c] += jnp.where(lane_ids == at, corr[v][:, x : x + 1], 0.0)

    def advance(sec, r, corr=None):
        coef_a, coef_b = COEFFS[sec]
        src, old = (state_ref, reg_ref) if sec == 0 else (u1_ref, reg_out_ref)
        dst = u1_ref if sec == 0 else out_ref
        step = step_ref[...]
        for v in range(NV):
            res = acc_ref[v, r, :]
            if corr is not None:
                res = res + corr[v]
            k = coef_a * old[v, r, :] + step * res
            reg_out_ref[v, r, :] = k
            dst[v, r, :] = src[v, r, :] + coef_b * k

    def advance_inner(sec):
        def one(t, carry):
            advance(sec, pl.ds(pl.multiple_of(t * SUB, SUB), SUB))
            return carry

        lax.fori_loop(tiles, (nx - 1) * tiles, one, 0)

    def advance_outer(u_ref, sec, side, t):
        x_copy(u_ref, sec, side, t).wait_recv()
        base = (0 if side == 0 else rows - ny) + t * SUB
        r = slice(base, base + SUB)
        own = [u_ref[v, r, :] for v in range(NV)]
        other = [xh_ref[sec, side, v, t * SUB : (t + 1) * SUB, :] for v in range(NV)]
        corr = face_terms(other, own, 0)[0] if side == 0 else face_terms(own, other, 0)[1]
        advance(sec, r, corr)

    def reduce_max(axis, top):
        for off in range(1, sizes[axis]):
            m_copy(axis, off).wait_recv()
            top = jnp.maximum(top, mx_ref[axis, off])
        return top

    def send_max(axis):
        for off in range(1, sizes[axis]):
            m_copy(axis, off).start()

    order = [(t, side) for t in range(tiles) for side in range(2)]
    for t, side in order:
        x_copy(state_ref, 0, side, t).start()
    top = pointwise(state_ref, True)
    mcur_ref[2] = top
    pack(state_ref, 0)
    send_max(2)
    for side in range(2):
        y_copy(0, side).start()
        z_copy(0, side).start()
    lax.fori_loop(0, NV, products, 0)
    top = reduce_max(2, top)
    mcur_ref[1] = top
    lax.fori_loop(0, NV * tiles, along_x, 0)
    send_max(1)
    dissipate(state_ref)
    top = reduce_max(1, top)
    mcur_ref[0] = top
    edges_y(0)
    send_max(0)
    edges_z(0)
    top = reduce_max(0, top)
    top = jnp.max(jnp.max(top, axis=0, keepdims=True), axis=1, keepdims=True)
    step_ref[...] = jnp.broadcast_to(COURANT * ELEM_WIDTH / (11.0 * top), (SUB, nz))
    for t, side in order:
        advance_outer(state_ref, 0, side, t)
        x_copy(u1_ref, 1, 1 - side, t).start()
    advance_inner(0)
    pack(u1_ref, 1)
    pointwise(u1_ref, False)
    for side in range(2):
        y_copy(1, side).start()
        z_copy(1, side).start()
    volume(u1_ref)
    edges_y(1)
    edges_z(1)
    advance_inner(1)
    for t, side in order:
        advance_outer(u1_ref, 1, 1 - side, t)
    for axis in range(3):
        for off in range(1, sizes[axis]):
            m_copy(axis, off).wait_send()
    for sec in range(2):
        for side in range(2):
            y_copy(sec, side).wait_send()
            z_copy(sec, side).wait_send()
            for t in range(tiles):
                x_copy(state_ref if sec == 0 else u1_ref, sec, side, t).wait_send()


def shards(sizes, state, register):
    nx, ny, nz = state.shape[1:]
    rows = nx * ny
    tiles = ny // SUB
    most = max(sizes)
    f32 = jnp.float32
    flat = (NV, rows, nz)
    ly = jnp.asarray(split(np.kron(np.eye(nx), operator(ny))))
    wz = jnp.asarray(split(windows(nz)))
    vmem = pl.BlockSpec(memory_space=pltpu.VMEM)
    dma = pltpu.SemaphoreType.DMA
    new_state, new_reg = pl.pallas_call(
        functools.partial(kernel, (nx, ny, nz), sizes),
        out_shape=[jax.ShapeDtypeStruct(flat, f32)] * 2,
        in_specs=[vmem] * 4,
        out_specs=[vmem] * 2,
        scratch_shapes=[
            pltpu.VMEM(flat, f32), pltpu.VMEM(flat, f32),
            pltpu.VMEM(flat, f32), pltpu.VMEM(flat, f32), pltpu.VMEM(flat, f32),
            pltpu.VMEM((rows, nz), f32), pltpu.VMEM((rows, nz), f32),
            pltpu.VMEM((SUB, nz), f32),
            pltpu.VMEM((2, 2, NV, ny, nz), f32),
            pltpu.VMEM((2, 2, NV, nx, nz), f32), pltpu.VMEM((2, 2, NV, nx, nz), f32),
            pltpu.VMEM((2, 2, NV, ny, LANE), f32), pltpu.VMEM((2, 2, NV, ny, LANE), f32),
            pltpu.VMEM((3, SUB, LANE), f32), pltpu.VMEM((3, most, SUB, LANE), f32),
            dma((2, 2, tiles)), dma((2, 2, tiles)), dma((2, 2)), dma((2, 2)),
            dma((2, 2)), dma((2, 2)), dma((3, most)), dma((3, most)),
        ],
        compiler_params=pltpu.CompilerParams(
            collective_id=0, has_side_effects=True, vmem_limit_bytes=48 * 1024 * 1024
        ),
        name="dg_step",
    )(state.reshape(flat), register.reshape(flat), ly, wz)
    return new_state.reshape(state.shape), new_reg.reshape(state.shape)


def solution(mesh):
    sizes = tuple(mesh.shape[a] for a in AXES)
    spec = P(None, "gx", "gy", "gz")
    return jax.shard_map(
        functools.partial(shards, sizes),
        mesh=mesh,
        in_specs=(spec, spec),
        out_specs=(spec, spec),
        check_vma=False,
    )
```

profile of v0, /device:TPU:0, one launch (start us, length us, event | category | flops | bytes accessed | tf_op | source)
XLA Modules:
  0.0 33.0 jit_solution(15846696913256919444)
XLA Ops:
  0.6 0.0 copy-start
  0.6 1.2 %copy-done = f32[5,6,24,384]{3,2,1,0:T(8,128)S(1)} copy-done((f32[5,6,24,384]{3,2,1,0:T(8,128)S(1)}, f32[5,6,24,384]{3,2,1,0:T(8,128)}, u32[]{:S(2)}) %copy-start) | copy-done | bytes 1105944
  1.9 0.0 copy-start.1
  1.9 1.2 %copy-done.1 = f32[5,6,24,384]{3,2,1,0:T(8,128)S(1)} copy-done((f32[5,6,24,384]{3,2,1,0:T(8,128)S(1)}, f32[5,6,24,384]{3,2,1,0:T(8,128)}, u32[]{:S(2)}) %copy-start.1) | copy-done | bytes 1105944
  3.1 0.0 copy-start.2
  3.1 1.0 %copy-done.2 = bf16[2,2,256,256]{3,2,1,0:T(8,128)(2,1)S(1)} copy-done((bf16[2,2,256,256]{3,2,1,0:T(8,128)(2,1)S(1)}, bf16[2,2,256,256]{3,2,1,0:T(8,128)(2,1)}, u32[]{:S(2)}) %copy-start.2) | copy-done | bytes 524312
  4.2 0.0 copy-start.3
  4.2 0.9 %copy-done.3 = bf16[2,144,144]{2,1,0:T(8,128)(2,1)S(1)} copy-done((bf16[2,144,144]{2,1,0:T(8,128)(2,1)S(1)}, bf16[2,144,144]{2,1,0:T(8,128)(2,1)}, u32[]{:S(2)}) %copy-start.3) | copy-done | bytes 82968
  5.1 26.0 %dg_step.1 = (f32[5,144,384]{2,1,0:T(8,128)S(1)}, f32[5,144,384]{2,1,0:T(8,128)S(1)}) custom-call(f32[5,144,384]{2,1,0:T(8,128)S(1)} %bitcast.4, f32[5,144,384]{2,1,0:T(8,128)S(1)} %bitcast.5, bf16[2,144,144]{2,1,0:T(8,128)(2,1)S(1)} %copy-done.3, bf16[2,2,256,256]{3,2,1,0:T(8,128)(2,1)S(1)} %copy-done.2), custom_call_target="tpu_custom_call" | custom-call | tf_op jit(solution)/shard_map/dg_step/pallas_call | solution.py:407
  31.0 1.0 %copy.8 = f32[5,6,24,384]{3,2,1,0:T(8,128)} copy(f32[5,6,24,384]{3,2,1,0:T(8,128)S(1)} %bitcast.7) | data formatting | bytes 2211840
  32.0 1.0 %copy.9 = f32[5,6,24,384]{3,2,1,0:T(8,128)} copy(f32[5,6,24,384]{3,2,1,0:T(8,128)S(1)} %bitcast.6) | data formatting | bytes 2211840
Async XLA Ops:
  0.6 1.2 %copy-start = (f32[5,6,24,384]{3,2,1,0:T(8,128)S(1)}, f32[5,6,24,384]{3,2,1,0:T(8,128)}, u32[]{:S(2)}) copy-start(f32[5,6,24,384]{3,2,1,0:T(8,128)} %param.4) | copy-start | bytes 3317764
  1.9 1.2 %copy-start.1 = (f32[5,6,24,384]{3,2,1,0:T(8,128)S(1)}, f32[5,6,24,384]{3,2,1,0:T(8,128)}, u32[]{:S(2)}) copy-start(f32[5,6,24,384]{3,2,1,0:T(8,128)} %param.5) | copy-start | bytes 3317764
  3.1 1.0 %copy-start.2 = (bf16[2,2,256,256]{3,2,1,0:T(8,128)(2,1)S(1)}, bf16[2,2,256,256]{3,2,1,0:T(8,128)(2,1)}, u32[]{:S(2)}) copy-start(bf16[2,2,256,256]{3,2,1,0:T(8,128)(2,1)} %constant.5.clone.wz_ref) | copy-start | bytes 1572868
  4.2 0.9 %copy-start.3 = (bf16[2,144,144]{2,1,0:T(8,128)(2,1)S(1)}, bf16[2,144,144]{2,1,0:T(8,128)(2,1)}, u32[]{:S(2)}) copy-start(bf16[2,144,144]{2,1,0:T(8,128)(2,1)} %constant.4.clone.ly_ref) | copy-start | bytes 248836
where the time goes:
time: 33.3 us; the launch traced here: 33 us
  Pallas kernels  26 us (78%)
  local copies, waits for them, and re-layouts  6.41 us (19%)
  between operations  0.65 us (2%)
    pallas_call x1, Pallas kernels, shards(): pl.pallas_call(functools.partial(kernel, (nx, ny, nz), sizes), out_shape=...  26 us
    unnamed x10, local copies, waits for them, and re-layouts  6.41 us

commit v1 on v0

--- a/solution.py
+++ b/solution.py
@@ -24,6 +24,7 @@
 NV = 5
 SUB = 8
 LANE = 128
+GRANT = 60 * 1024 * 1024
 MESH = pl.DeviceIdType.MESH
 
 
@@ -111,8 +112,9 @@
 
 def kernel(
     dims, sizes,
-    state_ref, reg_ref, ly_ref, wz_ref, out_ref, reg_out_ref,
-    u1_ref, acc_ref, fx_ref, fy_ref, fz_ref, sy_ref, sz_ref, step_ref,
+    state_hbm, reg_hbm, ly_hbm, wz_hbm, out_hbm, reg_out_hbm,
+    out_ref, reg_out_ref, save_sem,
+    state_ref, reg_ref, ly_ref, wz_ref, load_sem, u1_ref, acc_ref, fx_ref, fy_ref, fz_ref, sy_ref, sz_ref, step_ref,
     xh_ref, yp_ref, yh_ref, zp_ref, zh_ref, mcur_ref, mx_ref,
     xs_sem, xr_sem, ys_sem, yr_sem, zs_sem, zr_sem, ms_sem, mr_sem,
 ):
@@ -125,13 +127,21 @@
         n = sizes[axis]
         return {AXES[axis]: lax.rem(me[axis] + (offset % n), n)}
 
+    loads = [
+        pltpu.make_async_copy(src, dst, load_sem.at[i])
+        for i, (src, dst) in enumerate(
+            ((state_hbm, state_ref), (ly_hbm, ly_ref), (wz_hbm, wz_ref), (reg_hbm, reg_ref))
+        )
+    ]
+    for load in loads:
+        load.start()
+
     barrier = pltpu.get_barrier_semaphore()
     greeted = 0
     for axis in range(3):
         for off in range(1, sizes[axis]):
             pl.semaphore_signal(barrier, inc=1, device_id=peer(axis, off), device_id_type=MESH)
             greeted += 1
-    pl.semaphore_wait(barrier, greeted)
 
     def remote(src, dst, ssem, rsem, axis, off):
         return pltpu.make_async_remote_copy(
@@ -186,11 +196,11 @@
 
         lax.fori_loop(0, NV, one, 0)
 
-    def pointwise(u_ref, want_max):
-        def one(t, top):
+    def pointwise(u_ref, lo, hi):
+        def one(t, carry):
             r = pl.ds(pl.multiple_of(t * SUB, SUB), SUB)
             u = [u_ref[v, r, :] for v in range(NV)]
-            inv, mom_sq, press, sound = primitives(u)
+            inv, _, press, sound = primitives(u)
             for d, f_ref in enumerate((fx_ref, fy_ref, fz_ref)):
                 parts, vel = flux_of(u, d, inv, press)
                 for v in range(NV):
@@ -199,13 +209,21 @@
                     sy_ref[r, :] = jnp.abs(vel) + sound
                 if d == 2:
                     sz_ref[r, :] = jnp.abs(vel) + sound
-            if want_max:
-                speed = jnp.sqrt(mom_sq) * inv + sound
-                for b in range(nz // LANE):
-                    top = jnp.maximum(top, speed[:, b * LANE : (b + 1) * LANE])
+            return carry
+
+        lax.fori_loop(lo, hi, one, 0)
+
+    def local_max():
+        def one(t, top):
+            r = pl.ds(pl.multiple_of(t * SUB, SUB), SUB)
+            u = [state_ref[v, r, :] for v in range(NV)]
+            inv, mom_sq, _, sound = primitives(u)
+            speed = jnp.sqrt(mom_sq) * inv + sound
+            for b in range(nz // LANE):
+                top = jnp.maximum(top, speed[:, b * LANE : (b + 1) * LANE])
             return top
 
-        return lax.fori_loop(0, rows // SUB, one, jnp.zeros((SUB, LANE), jnp.float32))
+        return lax.fori_loop(0, nx * tiles, one, jnp.zeros((SUB, LANE), jnp.float32))
 
     def halves(x):
         high = x.astype(jnp.bfloat16)
@@ -344,44 +362,63 @@
             m_copy(axis, off).start()
 
     order = [(t, side) for t in range(tiles) for side in range(2)]
+    loads[0].wait()
+    top = local_max()
+    mcur_ref[0] = top
+    pack(state_ref, 0)
+    pl.semaphore_wait(barrier, greeted)
+    send_max(0)
     for t, side in order:
         x_copy(state_ref, 0, side, t).start()
-    top = pointwise(state_ref, True)
+    pointwise(state_ref, 0, nx * tiles)
+    top = reduce_max(0, top)
+    mcur_ref[1] = top
+    loads[1].wait()
+    loads[2].wait()
+    send_max(1)
+    lax.fori_loop(0, NV, products, 0)
+    top = reduce_max(1, top)
     mcur_ref[2] = top
-    pack(state_ref, 0)
+    loads[3].wait()
     send_max(2)
     for side in range(2):
         y_copy(0, side).start()
         z_copy(0, side).start()
-    lax.fori_loop(0, NV, products, 0)
+    lax.fori_loop(0, NV * tiles, along_x, 0)
+    dissipate(state_ref)
     top = reduce_max(2, top)
-    mcur_ref[1] = top
-    lax.fori_loop(0, NV * tiles, along_x, 0)
-    send_max(1)
-    dissipate(state_ref)
-    top = reduce_max(1, top)
-    mcur_ref[0] = top
-    edges_y(0)
-    send_max(0)
-    edges_z(0)
-    top = reduce_max(0, top)
     top = jnp.max(jnp.max(top, axis=0, keepdims=True), axis=1, keepdims=True)
     step_ref[...] = jnp.broadcast_to(COURANT * ELEM_WIDTH / (11.0 * top), (SUB, nz))
+    edges_y(0)
+    edges_z(0)
+    advance_inner(0)
+    pointwise(u1_ref, tiles, (nx - 1) * tiles)
     for t, side in order:
         advance_outer(state_ref, 0, side, t)
         x_copy(u1_ref, 1, 1 - side, t).start()
-    advance_inner(0)
     pack(u1_ref, 1)
-    pointwise(u1_ref, False)
+    pointwise(u1_ref, 0, tiles)
     for side in range(2):
         y_copy(1, side).start()
         z_copy(1, side).start()
+    pointwise(u1_ref, (nx - 1) * tiles, nx * tiles)
     volume(u1_ref)
     edges_y(1)
     edges_z(1)
     advance_inner(1)
+    saves = []
+
+    def save(lo, size):
+        for src, dst in ((out_ref, out_hbm), (reg_out_ref, reg_out_hbm)):
+            r = pl.ds(lo, size)
+            saves.append(pltpu.make_async_copy(src.at[:, r, :], dst.at[:, r, :], save_sem.at[len(saves)]))
+            saves[-1].start()
+
+    if nx > 2:
+        save(ny, rows - 2 * ny)
     for t, side in order:
         advance_outer(u1_ref, 1, 1 - side, t)
+        save((rows - ny if side == 0 else 0) + t * SUB, SUB)
     for axis in range(3):
         for off in range(1, sizes[axis]):
             m_copy(axis, off).wait_send()
@@ -391,6 +428,8 @@
             z_copy(sec, side).wait_send()
             for t in range(tiles):
                 x_copy(state_ref if sec == 0 else u1_ref, sec, side, t).wait_send()
+    for copy in saves:
+        copy.wait()
 
 
 def shards(sizes, state, register):
@@ -402,14 +441,16 @@
     flat = (NV, rows, nz)
     ly = jnp.asarray(split(np.kron(np.eye(nx), operator(ny))))
     wz = jnp.asarray(split(windows(nz)))
-    vmem = pl.BlockSpec(memory_space=pltpu.VMEM)
     dma = pltpu.SemaphoreType.DMA
     new_state, new_reg = pl.pallas_call(
         functools.partial(kernel, (nx, ny, nz), sizes),
         out_shape=[jax.ShapeDtypeStruct(flat, f32)] * 2,
-        in_specs=[vmem] * 4,
-        out_specs=[vmem] * 2,
+        in_specs=[pl.BlockSpec(memory_space=pltpu.HBM)] * 4,
+        out_specs=[pl.BlockSpec(memory_space=pl.ANY)] * 2,
         scratch_shapes=[
+            pltpu.VMEM(flat, f32), pltpu.VMEM(flat, f32), dma((2 + 4 * tiles,)),
+            pltpu.VMEM(flat, f32), pltpu.VMEM(flat, f32),
+            pltpu.VMEM(ly.shape, ly.dtype), pltpu.VMEM(wz.shape, wz.dtype), dma((4,)),
             pltpu.VMEM(flat, f32), pltpu.VMEM(flat, f32),
             pltpu.VMEM(flat, f32), pltpu.VMEM(flat, f32), pltpu.VMEM(flat, f32),
             pltpu.VMEM((rows, nz), f32), pltpu.VMEM((rows, nz), f32),
@@ -422,7 +463,7 @@
             dma((2, 2)), dma((2, 2)), dma((3, most)), dma((3, most)),
         ],
         compiler_params=pltpu.CompilerParams(
-            collective_id=0, has_side_effects=True, vmem_limit_bytes=48 * 1024 * 1024
+            collective_id=0, has_side_effects=True, vmem_limit_bytes=GRANT
         ),
         name="dg_step",
     )(state.reshape(flat), register.reshape(flat), ly, wz)

time: 33.3 us -> 31.8 us (0.955)
  local copies, waits for them, and re-layouts: 6.41 us -> 3.39 us
  Pallas kernels: 26 us -> 27.6 us
    unnamed x10 -> x4, local copies, waits for them, and re-layouts: 6.41 us -> 3.39 us
    pallas_call x1, Pallas kernels: 26 us -> 27.6 us  [shards(): pl.pallas_call(functools.partial(kernel, (nx, ny, nz), sizes), out_shape=...]
where the time goes in v1:
time: 31.8 us; the launch traced here: 31.7 us
  Pallas kernels  27.6 us (87%)
  local copies, waits for them, and re-layouts  3.39 us (11%)
  between operations  0.65 us (2%)
    pallas_call x1, Pallas kernels, shards(): pl.pallas_call(functools.partial(kernel, (nx, ny, nz), sizes), out_shape=...  27.6 us
    unnamed x4, local copies, waits for them, and re-layouts  3.39 us

profile of v1, /device:TPU:0, one launch (start us, length us, event | category | flops | bytes accessed | tf_op | source)
XLA Modules:
  0.0 31.7 jit_solution(8527322575751736600)
XLA Ops:
  0.6 27.6 %dg_step.1 = (f32[5,144,384]{2,1,0:T(8,128)}, f32[5,144,384]{2,1,0:T(8,128)}) custom-call(f32[5,144,384]{2,1,0:T(8,128)} %bitcast.4, f32[5,144,384]{2,1,0:T(8,128)} %bitcast.5, bf16[2,144,144]{2,1,0:T(8,128)(2,1)} %constant.4.clone.ly_hbm, bf16[2,2,256,256]{3,2,1,0:T(8,128)(2,1)} %constant.5.clone.wz_hbm), custom_call_target="tpu_custom_call" | custom-call | tf_op jit(solution)/shard_map/dg_step/pallas_call | solution.py:445
  28.3 0.0 copy-start
  28.3 2.4 %copy.8 = f32[5,6,24,384]{3,2,1,0:T(8,128)} copy(f32[5,6,24,384]{3,2,1,0:T(8,128)} %bitcast.7) | data formatting | bytes 2211840
  30.7 0.0 copy-done
  30.7 1.0 %copy.9 = f32[5,6,24,384]{3,2,1,0:T(8,128)} copy(f32[5,6,24,384]{3,2,1,0:T(8,128)S(1)} %bitcast.6) | data formatting | bytes 2211840
Async XLA Ops:
  28.3 2.4 %copy-start = (f32[5,144,384]{2,1,0:T(8,128)S(1)}, f32[5,144,384]{2,1,0:T(8,128)}, u32[]{:S(2)}) copy-start(f32[5,144,384]{2,1,0:T(8,128)} %get-tuple-element.5) | copy-start | bytes 3317764

commit v2 on v1

--- a/solution.py
+++ b/solution.py
@@ -362,14 +362,16 @@
             m_copy(axis, off).start()
 
     order = [(t, side) for t in range(tiles) for side in range(2)]
+    pl.semaphore_wait(barrier, greeted)
+    for t, side in order[:2]:
+        x_copy(state_hbm, 0, side, t).start()
     loads[0].wait()
     top = local_max()
     mcur_ref[0] = top
     pack(state_ref, 0)
-    pl.semaphore_wait(barrier, greeted)
     send_max(0)
-    for t, side in order:
-        x_copy(state_ref, 0, side, t).start()
+    for t, side in order[2:]:
+        x_copy(state_hbm, 0, side, t).start()
     pointwise(state_ref, 0, nx * tiles)
     top = reduce_max(0, top)
     mcur_ref[1] = top
@@ -386,11 +388,11 @@
         z_copy(0, side).start()
     lax.fori_loop(0, NV * tiles, along_x, 0)
     dissipate(state_ref)
+    edges_y(0)
+    edges_z(0)
     top = reduce_max(2, top)
     top = jnp.max(jnp.max(top, axis=0, keepdims=True), axis=1, keepdims=True)
     step_ref[...] = jnp.broadcast_to(COURANT * ELEM_WIDTH / (11.0 * top), (SUB, nz))
-    edges_y(0)
-    edges_z(0)
     advance_inner(0)
     pointwise(u1_ref, tiles, (nx - 1) * tiles)
     for t, side in order:
@@ -427,7 +429,7 @@
             y_copy(sec, side).wait_send()
             z_copy(sec, side).wait_send()
             for t in range(tiles):
-                x_copy(state_ref if sec == 0 else u1_ref, sec, side, t).wait_send()
+                x_copy(state_hbm if sec == 0 else u1_ref, sec, side, t).wait_send()
     for copy in saves:
         copy.wait()
 

time: 31.8 us -> 33.9 us (1.066)
  Pallas kernels: 27.6 us -> 29.8 us
    pallas_call x1, Pallas kernels: 27.6 us -> 29.8 us  [shards(): pl.pallas_call(functools.partial(kernel, (nx, ny, nz), sizes), out_shape=...]
where the time goes in v2:
time: 33.9 us; the launch traced here: 33.8 us
  Pallas kernels  29.8 us (88%)
  local copies, waits for them, and re-layouts  3.39 us (10%)
  between operations  0.65 us (2%)
    pallas_call x1, Pallas kernels, shards(): pl.pallas_call(functools.partial(kernel, (nx, ny, nz), sizes), out_shape=...  29.8 us
    unnamed x4, local copies, waits for them, and re-layouts  3.39 us

profile of v2, /device:TPU:0, one launch (start us, length us, event | category | flops | bytes accessed | tf_op | source)
XLA Modules:
  0.0 33.8 jit_solution(3331934647175998076)
XLA Ops:
  0.6 29.8 %dg_step.1 = (f32[5,144,384]{2,1,0:T(8,128)}, f32[5,144,384]{2,1,0:T(8,128)}) custom-call(f32[5,144,384]{2,1,0:T(8,128)} %bitcast.4, f32[5,144,384]{2,1,0:T(8,128)} %bitcast.5, bf16[2,144,144]{2,1,0:T(8,128)(2,1)} %constant.4.clone.ly_hbm, bf16[2,2,256,256]{3,2,1,0:T(8,128)(2,1)} %constant.5.clone.wz_hbm), custom_call_target="tpu_custom_call" | custom-call | tf_op jit(solution)/shard_map/dg_step/pallas_call | solution.py:447
  30.4 0.0 copy-start
  30.4 2.4 %copy.8 = f32[5,6,24,384]{3,2,1,0:T(8,128)} copy(f32[5,6,24,384]{3,2,1,0:T(8,128)} %bitcast.7) | data formatting | bytes 2211840
  32.8 0.0 copy-done
  32.8 1.0 %copy.9 = f32[5,6,24,384]{3,2,1,0:T(8,128)} copy(f32[5,6,24,384]{3,2,1,0:T(8,128)S(1)} %bitcast.6) | data formatting | bytes 2211840
Async XLA Ops:
  30.4 2.4 %copy-start = (f32[5,144,384]{2,1,0:T(8,128)S(1)}, f32[5,144,384]{2,1,0:T(8,128)}, u32[]{:S(2)}) copy-start(f32[5,144,384]{2,1,0:T(8,128)} %get-tuple-element.5) | copy-start | bytes 3317764
